TPU v7x, 32 devices: a whole 2x2x4 slice. The times are simulated.
32 devices in a mesh: seq: 8 (over z, y), head: 4 (over x, core).
Axes of the slice: x: 2, y: 2, z: 4, core: 2. Of those that a mesh axis runs over, the one named last changes fastest.
Arguments:
- query_rows: bfloat16 [8192, 4096], P('seq', 'head'), may hold values from -6 to 6
- key_rows: bfloat16 [8192, 1024], P('seq', 'head'), may hold values from -6 to 6
- value_rows: bfloat16 [8192, 1024], P('seq', 'head'), may hold values from -6 to 6
- attn_out: bfloat16 [8192, 4096], P('seq', 'head'), may hold values from -4 to 4
- out_grad: bfloat16 [8192, 4096], P(('seq', 'head')), may hold values from -6 to 6
- block_index: int32 [64, 8], P('seq'), may hold values from 0 to 63, as said below
- block_count: int32 [64], P('seq'), may hold values from 1 to 8
Outputs:
- query_grad: bfloat16 [8192, 4096], P('seq', 'head')
- key_grad: bfloat16 [8192, 1024], P('seq', 'head')
- value_grad: bfloat16 [8192, 1024], P('seq', 'head')
Inputs may be any that keep to these rules, and one draw needn't show every extreme that they name: `block_index`: row i lists distinct blocks, all at or before block i; its first entry is block i, and blocks i - 1, i - 2 and 0 are listed wherever they exist and differ from i. Entries at or past block_count[i] repeat block i. Counting with repetition the entries of the 8 query blocks of one index of seq that name blocks held by another index, leaving out block 0 and, for the index just below, its last two blocks: at most 4 for any pair of indices, and exactly 4 for some pair in every draw.
All inputs are finite; a program needn't handle non-finite values.
Results may differ from a plain program's by a relative error of at most 0.006.
Values may be sent and summed in bfloat16 or wider, within the bound.
A program may use at most 128 MiB of HBM per device.

v0:
```python
import jax
import jax.numpy as jnp
from jax import lax
from jax.sharding import PartitionSpec as P

HD = 128
GROUP = 4
BLK = 128
NF = 4


def shifted(value, axis, steps):
    count = lax.axis_size(axis)
    initial, last = (max(0, -steps), min(count, count - steps))
    return lax.ppermute(value, axis, [(source, source + steps) for source in range(initial, last)])


def broadcast(x, axis, root):
    mine = lax.axis_index(axis) == root
    return lax.psum(jnp.where(mine, x, jnp.zeros_like(x)), axis)


def plan_blocks(block_index, block_count, device, qblocks, seq_count, capacity):
    owner_dev = block_index // qblocks
    within = block_index % qblocks
    max_blocks = block_index.shape[1]
    is_live = jnp.arange(max_blocks, dtype=jnp.int32)[None, :] < block_count[:, None]
    is_local = owner_dev == device
    is_prev = (owner_dev == device - 1) & (within >= qblocks - 2)
    is_first = (block_index == 0) & jnp.logical_not(is_local) & jnp.logical_not(is_prev)
    is_far = (
        is_live & jnp.logical_not(is_local) & jnp.logical_not(is_prev) & jnp.logical_not(is_first)
    )
    flat_far = is_far.reshape(-1)
    flat_owner = owner_dev.reshape(-1)
    entries = flat_far.shape[0]
    entry_order = jnp.arange(entries, dtype=jnp.int32)
    earlier = (
        flat_far[None, :]
        & (flat_owner[None, :] == flat_owner[:, None])
        & (entry_order[None, :] < entry_order[:, None])
    )
    far_rank = jnp.sum(earlier.astype(jnp.int32), axis=1)
    far_slot = flat_owner * capacity + far_rank
    target_slot = jnp.where(flat_far, far_slot, seq_count * capacity)
    request = (
        jnp.zeros((seq_count * capacity + 1,), jnp.int32).at[target_slot].set(within.reshape(-1))
    )
    request = request[: seq_count * capacity].reshape(seq_count, capacity)
    far_position = qblocks + 3 + far_slot.reshape(block_index.shape)
    position = jnp.where(
        is_local,
        within,
        jnp.where(
            is_prev,
            qblocks + within - (qblocks - 2),
            jnp.where(is_first, qblocks + 2, far_position),
        ),
    )
    remote = (is_far | is_first & is_live).astype(jnp.int32)
    return (position, request, remote)


def local(query_rows, key_rows, value_rows, attn_out, out_grad, block_index, block_count):
    seq_count = lax.axis_size("seq")
    my_index = lax.axis_index("seq")
    grad_rows = lax.all_to_all(out_grad, "head", split_axis=1, concat_axis=0, tiled=True)
    qblocks = query_rows.shape[0] // BLK
    kv_heads = key_rows.shape[1] // HD
    max_blocks = block_index.shape[1]
    capacity = qblocks * NF // seq_count
    kv_width = 2 * kv_heads * HD
    kv_local = jnp.concatenate([key_rows, value_rows], axis=1).reshape(qblocks, BLK, kv_width)
    position, request, remote = plan_blocks(
        block_index, block_count, my_index, qblocks, seq_count, capacity
    )
    asked_rows = lax.all_to_all(request, "seq", split_axis=0, concat_axis=0, tiled=True)
    served = kv_local[asked_rows]
    fetched = lax.all_to_all(served, "seq", split_axis=0, concat_axis=0, tiled=True)
    prev_rows = shifted(kv_local[qblocks - 2 :], "seq", 1)
    first_rows = broadcast(kv_local[0:1], "seq", 0)
    kv_all = jnp.concatenate(
        [kv_local, prev_rows, first_rows, fetched.reshape(seq_count * capacity, BLK, kv_width)],
        axis=0,
    )
    slot_count = kv_all.shape[0]
    query_blocks = query_rows.reshape(qblocks, BLK, kv_heads, GROUP, HD)
    grad_blocks = grad_rows.reshape(qblocks, BLK, kv_heads, GROUP, HD)
    out_blocks = attn_out.reshape(qblocks, BLK, kv_heads, GROUP, HD)
    scale_factor = HD ** (-0.5)
    offsets = jnp.arange(BLK, dtype=jnp.int32)
    half_width = kv_width // 2

    def fetch_tiles(tile_position):
        gathered = kv_all[tile_position]
        count = tile_position.shape[0]
        key_tile = gathered[..., :half_width].reshape(count, BLK, kv_heads, HD)
        value_tile = gathered[..., half_width:].reshape(count, BLK, kv_heads, HD)
        return (key_tile, value_tile)

    def masked_scores(query_tile, key_tile, row_number, tile_index, live):
        scores = (
            jnp.einsum("rgqd,mcgd->gqrmc", query_tile, key_tile, preferred_element_type=jnp.float32)
            * scale_factor
        )
        query_pos = (my_index * qblocks + row_number) * BLK + offsets
        key_pos = tile_index[:, None] * BLK + offsets[None, :]
        allowed = live[:, None][None] & (key_pos[None] <= query_pos[:, None, None])
        return jnp.where(allowed, scores, -jnp.inf)

    def stats_of(masked):
        row_top = jnp.max(masked, axis=(3, 4), keepdims=True)
        row_total = jnp.sum(jnp.exp(masked - row_top), axis=(3, 4), keepdims=True)
        return (row_top, row_total)

    def terms_from(
        masked, row_top, row_total, query_tile, grad_tile, out_tile, key_tile, value_tile
    ):
        count = key_tile.shape[0]
        probs_full = jnp.exp(masked - row_top) / row_total
        probs_low = probs_full.astype(jnp.bfloat16)
        dprobs = jnp.einsum(
            "rgqd,mcgd->gqrmc", grad_tile, value_tile, preferred_element_type=jnp.float32
        )
        out_dot = jnp.sum(grad_tile.astype(jnp.float32) * out_tile.astype(jnp.float32), axis=-1)
        out_dot = jnp.transpose(out_dot, (1, 2, 0))[..., None, None]
        dscores_low = (probs_full * (dprobs - out_dot)).astype(jnp.bfloat16)
        query_grad_tile = (
            jnp.einsum(
                "gqrmc,mcgd->rgqd", dscores_low, key_tile, preferred_element_type=jnp.float32
            )
            * scale_factor
        )
        key_part = (
            jnp.einsum(
                "gqrmc,rgqd->mcgd", dscores_low, query_tile, preferred_element_type=jnp.float32
            )
            * scale_factor
        )
        value_part = jnp.einsum(
            "gqrmc,rgqd->mcgd", probs_low, grad_tile, preferred_element_type=jnp.float32
        )
        update = jnp.concatenate(
            [key_part.reshape(count, BLK, half_width), value_part.reshape(count, BLK, half_width)],
            axis=-1,
        )
        return (query_grad_tile.reshape(BLK, -1), update)

    zeros_acc = jnp.zeros((slot_count, BLK, kv_width), jnp.float32)
    row_numbers = jnp.arange(qblocks, dtype=jnp.int32)
    entry_ids = jnp.arange(max_blocks, dtype=jnp.int32)
    live_all = entry_ids[None, :] < block_count[:, None]

    def one_block(accumulated, inputs):
        row_number, query_tile, grad_tile, out_tile, tile_index, tile_live, tile_position = inputs
        key_tile, value_tile = fetch_tiles(tile_position)
        masked = masked_scores(query_tile, key_tile, row_number, tile_index, tile_live)
        row_top, row_total = stats_of(masked)
        query_part, update = terms_from(
            masked, row_top, row_total, query_tile, grad_tile, out_tile, key_tile, value_tile
        )
        return (accumulated.at[tile_position].add(update), query_part.astype(jnp.bfloat16))

    inputs = (row_numbers, query_blocks, grad_blocks, out_blocks, block_index, live_all, position)
    accumulated, query_grad = lax.scan(one_block, zeros_acc, inputs)
    far_part = accumulated[qblocks + 3 :].reshape(seq_count, capacity, BLK, kv_width)
    returned = lax.all_to_all(far_part, "seq", split_axis=0, concat_axis=0, tiled=True)
    own_grad = accumulated[:qblocks]
    returned_prev = shifted(
        accumulated[qblocks : qblocks + 2].astype(jnp.bfloat16), "seq", -1
    ).astype(jnp.float32)
    own_grad = own_grad.at[qblocks - 2 :].add(returned_prev)
    selector = (
        asked_rows.reshape(-1)[None, :] == jnp.arange(qblocks, dtype=jnp.int32)[:, None]
    ).astype(jnp.float32)
    far_terms = returned.reshape(seq_count * capacity, BLK * kv_width)
    own_grad = own_grad + jnp.dot(selector, far_terms, precision=lax.Precision.HIGHEST).reshape(
        qblocks, BLK, kv_width
    )
    first_total = lax.psum(accumulated[qblocks + 2], "seq")
    own_grad = own_grad.at[0].add(
        jnp.where(my_index == 0, first_total, jnp.zeros_like(first_total))
    )
    key_grad = own_grad[..., :half_width].reshape(qblocks * BLK, half_width).astype(jnp.bfloat16)
    value_grad = own_grad[..., half_width:].reshape(qblocks * BLK, half_width).astype(jnp.bfloat16)
    return (query_grad.reshape(qblocks * BLK, -1), key_grad, value_grad)


def solution(mesh):
    return jax.shard_map(
        local,
        mesh=mesh,
        in_specs=(
            P("seq", "head"),
            P("seq", "head"),
            P("seq", "head"),
            P("seq", "head"),
            P(("seq", "head"), None),
            P("seq", None),
            P("seq"),
        ),
        out_specs=(P("seq", "head"), P("seq", "head"), P("seq", "head")),
        check_vma=False,
    )
```

profile of v0, /device:TPU:0, one launch (start us, length us, event | category | flops | bytes accessed | tf_op | source)
XLA Modules:
  0.0 647.8 jit_solution(7845131346142039962)
XLA Ops:
  11.5 7.3 %all-to-all-start = ((s32[8,1,4]{2,1,0:T(1,128)}), s32[8,1,4]{2,1,0:T(1,128)S(1)}, u32[]{:S(2)}, u32[]{:S(2)}) async-start(s32[8,1,4]{2,1,0:T(1,128)} %bitcast.5), calls=%async_computation | async-start | bytes 8192 | tf_op jit(solution)/shard_map/all_to_all | solution.py:77
  22.0 3.3 all-to-all-done
  25.2 3.6 all-to-all-start.2
  34.1 20.4 %all-to-all-done.2 = bf16[256,4,1024]{2,0,1:T(8,128)(2,1)S(1)} async-done(((bf16[256,4,1024]{2,0,1:T(8,128)(2,1)}), bf16[256,4,1024]{2,0,1:T(8,128)(2,1)S(1)}, u32[]{:S(2)}, u32[]{:S(2)}) %all-to-all-start.2) | async-done | bytes 2097184 | tf_op jit(solution)/shard_map/all_to_all | solution.py:67
  54.5 4.6 all-to-all-start.1
  59.8 3.8 collective-permute-start
  64.3 4.4 reshape.378
  68.7 4.5 reshape.379
  75.9 102.6 %all-reduce.3.cloned.1.call-done = bf16[1,128,512]{2,1,0:T(8,128)(2,1)} async-done(((bf16[1,128,512]{2,1,0:T(8,128)(2,1)}), bf16[1,128,512]{2,1,0:T(8,128)(2,1)}) %all-reduce.3.cloned.1.call-update) | async-done | bytes 131088 | tf_op jit(solution)/shard_map/psum | solution.py:20
  178.5 7.0 %pad_maximum_fusion.1 = bf16[43,128,512]{2,1,0:T(8,128)(2,1)} fusion(bf16[32,128,512]{2,1,0:T(8,128)(2,1)} %bitcast.8, bf16[1,128,512]{2,1,0:T(8,128)(2,1)} %all-reduce.3.cloned.1.call-done, bf16[2,128,512]{2,1,0:T(8,128)(2,1)S(1)} %collective-permute-done, bf16[8,128,512]{2,1,0:T(8,128)(2,1)S(1)} %bitcast.206), kind=kLoop, calls=%fused_computation.58 | loop fusion | flops 8454144 | bytes 11272192 | tf_op jit(solution)/shard_map/concatenate | solution.py:82
  185.5 5.6 broadcast_in_dim.31
  191.1 187.3 %while.18 = (s32[]{:T(128)}, f32[43,128,512]{2,1,0:T(8,128)}, bf16[8,128,1024]{2,1,0:T(8,128)(2,1)}, s32[8,8]{1,0:T(8,128)S(1)}, bf16[8,128,2,4,128]{4,3,2,1,0:T...) while((s32[]{:T(128)}, f32[43,128,512]{2,1,0:T(8,128)}, ...), condition=%wide.region_8.9_spmd.clone.clone, body=%wide.region_3.8_spmd.clone.clone.sunk | while | flops 1364458624 | bytes 57066980 | solution.py:165
  195.9 3.2 gather_fusion
  210.2 4.2 scatter_fusion
  219.2 3.2 gather_fusion
  233.6 4.4 scatter_fusion
  242.7 3.2 gather_fusion
  257.0 4.5 scatter_fusion
  280.6 4.5 scatter_fusion
  304.2 4.3 scatter_fusion
  313.3 3.2 gather_fusion
  327.6 4.1 scatter_fusion
  336.5 3.2 gather_fusion
  350.8 4.2 scatter_fusion
  359.7 3.2 gather_fusion
  374.1 4.4 scatter_fusion
  378.5 8.2 %slice.98 = f32[32,128,512]{2,1,0:T(8,128)} slice(f32[43,128,512]{2,1,0:T(8,128)} %get-tuple-element.181), slice={[11:43], [0:128], [0:512]} | slice | bytes 16777216 | tf_op jit(solution)/shard_map/slice | solution.py:166
  386.7 4.9 all-to-all-start.3
  397.0 15.4 %copy.156 = f32[43,128,512]{2,0,1:T(8,128)} copy(f32[43,128,512]{2,1,0:T(8,128)} %get-tuple-element.181) | data formatting | bytes 22544384 | tf_op jit(solution)/shard_map/while | solution.py:165
  412.4 201.8 %all-reduce.5.cloned.1.call-done = f32[128,512]{1,0:T(8,128)} async-done(((f32[128,512]{1,0:T(8,128)}), f32[128,512]{1,0:T(8,128)}) %all-reduce.5.cloned.1.call-update) | async-done | bytes 262160 | tf_op jit(solution)/shard_map/psum | solution.py:180
  616.9 12.4 %fusion.44 = f32[8,128,512]{2,0,1:T(8,128)S(1)} fusion(f32[8,128,512]{2,0,1:T(8,128)S(1)} %copy_dynamic-update-slice_fusion, s32[32]{0:T(128)S(1)} %eq.62, f32[4,8,128,512]{3,2,1,0:T(8,128)} %bitcast.70), kind=kOutput, calls=%fused_computation.60 | convolution fusion | flops 201851136 | bytes 12583040 | tf_op jit(solution)/shard_map/dot_general | solution.py:177
  631.1 6.3 scatter-add.20
  (263 shorter events, 157.4 us)
Async XLA Ops:
  11.5 13.7 %all-to-all-start = ((s32[8,1,4]{2,1,0:T(1,128)}), s32[8,1,4]{2,1,0:T(1,128)S(1)}, u32[]{:S(2)}, u32[]{:S(2)}) async-start(s32[8,1,4]{2,1,0:T(1,128)} %bitcast.5), calls=%async_computation | async-start | bytes 8192 | tf_op jit(solution)/shard_map/all_to_all | solution.py:77
  25.2 29.3 %all-to-all-start.2 = ((bf16[256,4,1024]{2,0,1:T(8,128)(2,1)}), bf16[256,4,1024]{2,0,1:T(8,128)(2,1)S(1)}, u32[]{:S(2)}, u32[]{:S(2)}) async-start(bf16[256,4,1024]{2,0,1:T(8,128)(2,1)} %bitcast.211), calls=%async_computation.2 | async-start | bytes 4194304 | tf_op jit(solution)/shard_map/all_to_all | solution.py:67
  54.5 124.0 %all-to-all-start.1 = ((bf16[8,4,128,512]{3,2,1,0:T(8,128)(2,1)}), bf16[8,4,128,512]{3,2,1,0:T(8,128)(2,1)}, u32[]{:S(2)}, u32[]{:S(2)}) async-start(bf16[8,4,128,512]{3,2,1,0:T(8,128)(2,1)} %bitcast.208), calls=%async_computation.1 | async-start | bytes 8388608 | tf_op jit(solution)/shard_map/all_to_all | solution.py:79
  59.1 119.5 %all-reduce.3.cloned.1.call-start = ((), (), s32[]{:S(2)}) async-start(), calls=%async_computation.4 | async-start | bytes 262144 | tf_op jit(solution)/shard_map/psum | solution.py:20
  59.8 118.7 %collective-permute-start = (bf16[2,128,512]{2,1,0:T(8,128)(2,1)}, bf16[2,128,512]{2,1,0:T(8,128)(2,1)S(1)}, u32[]{:S(2)}, u32[]{:S(2)}) collective-permute-start(bf16[2,128,512]{2,1,0:T(8,128)(2,1)} %bitcast.1), channel_id=1, source_target_pairs={{0,4},{4,8},{8,12},{12,16},{16,20},{20,24},{24,28},{1,5},{5,9},{9,... | collective-permute-start | bytes 786440 | tf_op jit(solution)/shard_map/ppermute | solution.py:15
  386.7 230.2 %all-to-all-start.3 = ((f32[8,4,128,512]{3,2,1,0:T(8,128)}), f32[8,4,128,512]{3,2,1,0:T(8,128)}, u32[]{:S(2)}, u32[]{:S(2)}) async-start(f32[8,4,128,512]{3,2,1,0:T(8,128)} %bitcast.207), calls=%async_computation.3 | async-start | bytes 16777216 | tf_op jit(solution)/shard_map/all_to_all | solution.py:167
  391.6 222.6 %all-reduce.5.cloned.1.call-start = ((), (), s32[]{:S(2)}) async-start(), calls=%async_computation.5 | async-start | bytes 524288 | tf_op jit(solution)/shard_map/psum | solution.py:180
  394.5 220.7 %collective-permute-start.1 = (bf16[2,128,512]{2,1,0:T(8,128)(2,1)S(1)}, bf16[2,128,512]{2,1,0:T(8,128)(2,1)S(1)}, u32[]{:S(2)}, u32[]{:S(2)}) collective-permute-start(bf16[2,128,512]{2,1,0:T(8,128)(2,1)S(1)} %slice.127), channel_id=1, source_target_pairs={{4,0},{8,4},{12,8},{16,12},{20,16},{24,20},{28,24},{5,1},{9,5},{13... | collective-permute-start | bytes 786440 | tf_op jit(solution)/shard_map/ppermute | solution.py:15
  412.4 203.9 %slice-start = ((f32[43,128,512]{2,0,1:T(8,128)}), f32[8,128,512]{2,0,1:T(8,128)S(1)}, s32[]{:S(2)}) async-start(f32[43,128,512]{2,0,1:T(8,128)} %copy.156), calls=%async_computation.6 | async-start | bytes 4194304 | tf_op jit(solution)/shard_map/slice | solution.py:168
  629.4 1.3 copy-start
Sparse Core Ops, SparseCore 0:
  64.4 114.0 all-reduce.2
  396.4 217.7 all-reduce.4
where the time goes:
time: 651 us; the launch traced here: 648 us
  waiting for transfers between devices  328 us (50%)
  local copies, waits for them, and re-layouts  143 us (22%)
  other arithmetic  78.1 us (12%)
  matrix products  53 us (8%)
  starting transfers between devices  25.5 us (4%)
  between operations  14.2 us (2%)
    psum x1, waiting for transfers between devices, local(): first_total = lax.psum(accumulated[qblocks + 2], 'seq')  202 us
    psum x1, waiting for transfers between devices, broadcast(): return lax.psum(jnp.where(mine, x, jnp.zeros_like(x)), axis)  103 us
    scatter-add x8, other arithmetic, one_block(): accumulated.at[tile_position].add(update)  34.5 us
    gather x8, local copies, waits for them, and re-layouts, fetch_tiles(): gathered = kv_all[tile_position]  25.7 us
    dynamic_slice x24, local copies, waits for them, and re-layouts, local(): accumulated, query_grad = lax.scan(one_block, zeros_acc, inputs)  22.8 us
    all_to_all x1, waiting for transfers between devices, local(): lax.all_to_all(out_grad, 'head', split_axis=1, concat_axis=0, tiled=True)  20.4 us
    while x1, local copies, waits for them, and re-layouts, local(): accumulated, query_grad = lax.scan(one_block, zeros_acc, inputs)  15.4 us
    concatenate x8, local copies, waits for them, and re-layouts, terms_from(): jnp.concatenate([key_part.reshape(count, BLK, half_width), value_part.res...  15.3 us
  transfers between devices with their start and end apart: 8, of which 4 were waited for; matrix products, arithmetic and copies ran while one was open for 7% of the time, Pallas kernels for 0%

commit v1 on v0

--- a/solution.py
+++ b/solution.py
@@ -17,7 +17,7 @@
 
 def broadcast(x, axis, root):
     mine = lax.axis_index(axis) == root
-    return lax.psum(jnp.where(mine, x, jnp.zeros_like(x)), axis)
+    return jnp.sum(lax.all_gather(jnp.where(mine, x, jnp.zeros_like(x)), axis), axis=0)
 
 
 def plan_blocks(block_index, block_count, device, qblocks, seq_count, capacity):

time: 651 us -> 642 us (0.986)
  waiting for transfers between devices: 328 us -> 317 us
    psum x1 -> x0, waiting for transfers between devices: 103 us -> none  [broadcast(): return lax.psum(jnp.where(mine, x, jnp.zeros_like(x)), axis)]
    all_gather x0 -> x1, waiting for transfers between devices: none -> 89.5 us  [broadcast(): lax.all_gather(jnp.where(mine, x, jnp.zeros_like(x)), axis)]
where the time goes in v1:
time: 642 us; the launch traced here: 639 us
  waiting for transfers between devices  317 us (49%)
  local copies, waits for them, and re-layouts  143 us (22%)
  other arithmetic  79.4 us (12%)
  matrix products  52.9 us (8%)
  starting transfers between devices  26.8 us (4%)
  between operations  14.2 us (2%)
    psum x1, waiting for transfers between devices, local(): first_total = lax.psum(accumulated[qblocks + 2], 'seq')  204 us
    all_gather x1, waiting for transfers between devices, broadcast(): lax.all_gather(jnp.where(mine, x, jnp.zeros_like(x)), axis)  89.5 us
    scatter-add x8, other arithmetic, one_block(): accumulated.at[tile_position].add(update)  34.5 us
    gather x8, local copies, waits for them, and re-layouts, fetch_tiles(): gathered = kv_all[tile_position]  25.7 us
    dynamic_slice x24, local copies, waits for them, and re-layouts, local(): accumulated, query_grad = lax.scan(one_block, zeros_acc, inputs)  22.8 us
    all_to_all x1, waiting for transfers between devices, local(): lax.all_to_all(out_grad, 'head', split_axis=1, concat_axis=0, tiled=True)  20.4 us
    while x1, local copies, waits for them, and re-layouts, local(): accumulated, query_grad = lax.scan(one_block, zeros_acc, inputs)  15.4 us
    concatenate x8, local copies, waits for them, and re-layouts, terms_from(): jnp.concatenate([key_part.reshape(count, BLK, half_width), value_part.res...  15.3 us
  transfers between devices with their start and end apart: 8, of which 4 were waited for; matrix products, arithmetic and copies ran while one was open for 7% of the time, Pallas kernels for 0%

profile of v1, /device:TPU:0, one launch (start us, length us, event | category | flops | bytes accessed | tf_op | source)
XLA Modules:
  0.0 639.1 jit_solution(2107556633249665519)
XLA Ops:
  11.5 7.3 %all-to-all-start = ((s32[8,1,4]{2,1,0:T(1,128)}), s32[8,1,4]{2,1,0:T(1,128)S(1)}, u32[]{:S(2)}, u32[]{:S(2)}) async-start(s32[8,1,4]{2,1,0:T(1,128)} %bitcast.6), calls=%async_computation | async-start | bytes 8192 | tf_op jit(solution)/shard_map/all_to_all | solution.py:77
  22.0 3.3 all-to-all-done
  25.2 3.6 all-to-all-start.2
  34.1 20.4 %all-to-all-done.2 = bf16[256,4,1024]{2,0,1:T(8,128)(2,1)S(1)} async-done(((bf16[256,4,1024]{2,0,1:T(8,128)(2,1)}), bf16[256,4,1024]{2,0,1:T(8,128)(2,1)S(1)}, u32[]{:S(2)}, u32[]{:S(2)}) %all-to-all-start.2) | async-done | bytes 2097184 | tf_op jit(solution)/shard_map/all_to_all | solution.py:67
  54.5 4.6 all-to-all-start.1
  60.5 3.8 collective-permute-start
  64.3 4.4 reshape.382
  68.8 4.5 reshape.383
  76.0 89.5 %all-gather.3.cloned.1.call-done = bf16[1024,512]{1,0:T(8,128)(2,1)} async-done(((bf16[128,512]{1,0:T(8,128)(2,1)}), bf16[1024,512]{1,0:T(8,128)(2,1)}) %all-gather.3.cloned.1.call-update) | async-done | bytes 1048592 | tf_op jit(solution)/shard_map/all_gather | solution.py:20
  166.8 6.9 %pad_maximum_fusion.1 = bf16[43,128,512]{2,1,0:T(8,128)(2,1)} fusion(bf16[32,128,512]{2,1,0:T(8,128)(2,1)} %bitcast.9, bf16[1,128,512]{2,1,0:T(8,128)(2,1)S(1)} %bitcast.215, bf16[2,128,512]{2,1,0:T(8,128)(2,1)S(1)} %collective-permute-done, bf16[8,128,512]{2,1,0:T(8,128)(2,1)S(1)} %bitcast.206), kind=kLoop, calls=%fused_computation.58 | loop fusion | flops 8454144 | bytes 11272192 | tf_op jit(solution)/shard_map/concatenate | solution.py:82
  173.8 5.6 broadcast_in_dim.31
  179.4 187.3 %while.18 = (s32[]{:T(128)}, f32[43,128,512]{2,1,0:T(8,128)}, bf16[8,128,1024]{2,1,0:T(8,128)(2,1)}, s32[8,8]{1,0:T(8,128)S(1)}, bf16[8,128,2,4,128]{4,3,2,1,0:T...) while((s32[]{:T(128)}, f32[43,128,512]{2,1,0:T(8,128)}, ...), condition=%wide.region_8.9_spmd.clone.clone, body=%wide.region_3.8_spmd.clone.clone.sunk | while | flops 1364458624 | bytes 57066980 | solution.py:165
  184.1 3.2 gather_fusion
  198.5 4.2 scatter_fusion
  221.8 4.4 scatter_fusion
  230.9 3.2 gather_fusion
  245.3 4.5 scatter_fusion
  254.5 3.2 gather_fusion
  268.8 4.5 scatter_fusion
  278.1 3.2 gather_fusion
  292.4 4.3 scatter_fusion
  315.8 4.1 scatter_fusion
  324.7 3.2 gather_fusion
  339.0 4.2 scatter_fusion
  347.9 3.2 gather_fusion
  362.3 4.4 scatter_fusion
  366.7 8.2 %slice.98 = f32[32,128,512]{2,1,0:T(8,128)} slice(f32[43,128,512]{2,1,0:T(8,128)} %get-tuple-element.181), slice={[11:43], [0:128], [0:512]} | slice | bytes 16777216 | tf_op jit(solution)/shard_map/slice | solution.py:166
  374.9 6.2 all-to-all-start.3
  386.4 15.4 %copy.156 = f32[43,128,512]{2,0,1:T(8,128)} copy(f32[43,128,512]{2,1,0:T(8,128)} %get-tuple-element.181) | data formatting | bytes 22544384 | tf_op jit(solution)/shard_map/while | solution.py:165
  401.8 203.7 %all-reduce.2.cloned.1.call-done = f32[128,512]{1,0:T(8,128)} async-done(((f32[128,512]{1,0:T(8,128)}), f32[128,512]{1,0:T(8,128)}) %all-reduce.2.cloned.1.call-update) | async-done | bytes 262160 | tf_op jit(solution)/shard_map/psum | solution.py:180
  608.2 12.4 %fusion.44 = f32[8,128,512]{2,0,1:T(8,128)S(1)} fusion(f32[8,128,512]{2,0,1:T(8,128)S(1)} %copy_dynamic-update-slice_fusion, s32[32]{0:T(128)S(1)} %eq.62, f32[4,8,128,512]{3,2,1,0:T(8,128)} %bitcast.71), kind=kOutput, calls=%fused_computation.60 | convolution fusion | flops 201851136 | bytes 12583040 | tf_op jit(solution)/shard_map/dot_general | solution.py:177
  622.3 6.3 scatter-add.20
  (264 shorter events, 158.8 us)
Async XLA Ops:
  11.5 13.7 %all-to-all-start = ((s32[8,1,4]{2,1,0:T(1,128)}), s32[8,1,4]{2,1,0:T(1,128)S(1)}, u32[]{:S(2)}, u32[]{:S(2)}) async-start(s32[8,1,4]{2,1,0:T(1,128)} %bitcast.6), calls=%async_computation | async-start | bytes 8192 | tf_op jit(solution)/shard_map/all_to_all | solution.py:77
  25.2 29.3 %all-to-all-start.2 = ((bf16[256,4,1024]{2,0,1:T(8,128)(2,1)}), bf16[256,4,1024]{2,0,1:T(8,128)(2,1)S(1)}, u32[]{:S(2)}, u32[]{:S(2)}) async-start(bf16[256,4,1024]{2,0,1:T(8,128)(2,1)} %bitcast.211), calls=%async_computation.2 | async-start | bytes 4194304 | tf_op jit(solution)/shard_map/all_to_all | solution.py:67
  54.5 112.3 %all-to-all-start.1 = ((bf16[8,4,128,512]{3,2,1,0:T(8,128)(2,1)}), bf16[8,4,128,512]{3,2,1,0:T(8,128)(2,1)}, u32[]{:S(2)}, u32[]{:S(2)}) async-start(bf16[8,4,128,512]{3,2,1,0:T(8,128)(2,1)} %bitcast.208), calls=%async_computation.1 | async-start | bytes 8388608 | tf_op jit(solution)/shard_map/all_to_all | solution.py:79
  59.1 106.4 %all-gather.3.cloned.1.call-start = ((), (), s32[]{:S(2)}) async-start(), calls=%async_computation.5 | async-start | bytes 1179648 | tf_op jit(solution)/shard_map/all_gather | solution.py:20
  60.5 106.3 %collective-permute-start = (bf16[2,128,512]{2,1,0:T(8,128)(2,1)}, bf16[2,128,512]{2,1,0:T(8,128)(2,1)S(1)}, u32[]{:S(2)}, u32[]{:S(2)}) collective-permute-start(bf16[2,128,512]{2,1,0:T(8,128)(2,1)} %bitcast.1), channel_id=1, source_target_pairs={{0,4},{4,8},{8,12},{12,16},{16,20},{20,24},{24,28},{1,5},{5,9},{9,... | collective-permute-start | bytes 786440 | tf_op jit(solution)/shard_map/ppermute | solution.py:15
  374.9 233.3 %all-to-all-start.3 = ((f32[8,4,128,512]{3,2,1,0:T(8,128)}), f32[8,4,128,512]{3,2,1,0:T(8,128)}, u32[]{:S(2)}, u32[]{:S(2)}) async-start(f32[8,4,128,512]{3,2,1,0:T(8,128)} %bitcast.207), calls=%async_computation.3 | async-start | bytes 16777216 | tf_op jit(solution)/shard_map/all_to_all | solution.py:167
  381.1 224.4 %all-reduce.2.cloned.1.call-start = ((), (), s32[]{:S(2)}) async-start(), calls=%async_computation.4 | async-start | bytes 524288 | tf_op jit(solution)/shard_map/psum | solution.py:180
  383.9 222.6 %collective-permute-start.1 = (bf16[2,128,512]{2,1,0:T(8,128)(2,1)S(1)}, bf16[2,128,512]{2,1,0:T(8,128)(2,1)S(1)}, u32[]{:S(2)}, u32[]{:S(2)}) collective-permute-start(bf16[2,128,512]{2,1,0:T(8,128)(2,1)S(1)} %slice.125), channel_id=1, source_target_pairs={{4,0},{8,4},{12,8},{16,12},{20,16},{24,20},{28,24},{5,1},{9,5},{13... | collective-permute-start | bytes 786440 | tf_op jit(solution)/shard_map/ppermute | solution.py:15
  401.8 205.8 %slice-start = ((f32[43,128,512]{2,0,1:T(8,128)}), f32[8,128,512]{2,0,1:T(8,128)S(1)}, s32[]{:S(2)}) async-start(f32[43,128,512]{2,0,1:T(8,128)} %copy.156), calls=%async_computation.6 | async-start | bytes 4194304 | tf_op jit(solution)/shard_map/slice | solution.py:168
  620.6 1.3 copy-start
Sparse Core Ops, SparseCore 0:
  62.6 102.8 all-gather.2
  385.8 219.6 all-reduce.1
